TPU v7x, 32 devices: a whole 2x2x4 slice. The times are simulated.
32 devices in a mesh: gy: 16 (over z, y, core), gz: 2 (over x).
Axes of the slice: x: 2, y: 2, z: 4, core: 2. Of those that a mesh axis runs over, the one named last changes fastest.
Arguments:
- scalar: float32 [8, 384, 384], P('gz', 'gy'), may hold values from -6 to 6
- velocity: float32 [3, 8, 128, 128], P(None, None, 'gy', 'gz'), may hold values from -0.9 to 0.9
Outputs:
- remeshed: float32 [8, 384, 384], P('gz', 'gy')
All inputs are finite; a program needn't handle non-finite values.
Results may differ from a plain program's by a relative error of at most 0.0003.
Values sent between devices are 32-bit elements; how exact they have to be, the bound alone decides.
A program may use at most 64 MiB of HBM per device.

v0:
```python
import jax
import jax.numpy as jnp
from jax import lax
from jax.sharding import PartitionSpec as P


def padded_2(value, sides, width):
    for axis, dim in sides:
        peers, length = (lax.axis_size(axis), value.shape[dim])
        up = [(i, (i + 1) % peers) for i in range(peers - 1)]
        down = [(j, i) for i, j in up]
        last = lax.slice_in_dim(value, length - width, length, axis=dim)
        initial = lax.slice_in_dim(value, 0, width, axis=dim)
        before = lax.ppermute(last, axis, up)
        after = lax.ppermute(initial, axis, down)
        value = jnp.concatenate([before, value, after], axis=dim)
    return value


def passed_along(block, axis, distance):
    devices = range(lax.axis_size(axis))
    route = [((i - distance) % len(devices), i) for i in devices]
    return lax.ppermute(block, axis, route)


def alternate(current, following, along):
    pieces = [current * (1.0 - phase / 3.0) + following * (phase / 3.0) for phase in range(3)]
    stacked = jnp.stack(pieces, axis=along + 1)
    new_shape = list(current.shape)
    new_shape[along] = new_shape[along] * 3
    return stacked.reshape(new_shape)


def polynomial(factors, value):
    result = jnp.zeros_like(value)
    for factor in reversed(factors):
        result = result * value + factor
    return result


def kernel_weight(offset):
    size = jnp.abs(offset)
    inner = polynomial([1.0, 0.0, -5.0 / 4.0, -35.0 / 12.0, 21.0 / 4.0, -25.0 / 12.0], size)
    middle = polynomial(
        [-4.0, 75.0 / 4.0, -245.0 / 8.0, 545.0 / 24.0, -63.0 / 8.0, 25.0 / 24.0], size
    )
    outer = polynomial(
        [18.0, -153.0 / 4.0, 255.0 / 8.0, -313.0 / 24.0, 21.0 / 8.0, -5.0 / 24.0], size
    )
    return jnp.where(
        size < 1.0, inner, jnp.where(size < 2.0, middle, jnp.where(size < 3.0, outer, 0.0))
    )


def displacement(speed, before, after):
    half_step = 0.5 * speed
    return jnp.where(
        half_step >= 0.0,
        (1.0 - half_step) * speed + half_step * after,
        (1.0 + half_step) * speed - half_step * before,
    )


def sweep_periodic(field, speed, along):
    moved = displacement(speed, jnp.roll(speed, 1, along), jnp.roll(speed, -1, along))
    result = jnp.zeros_like(field)
    for offset in range(-3, 4):
        result = result + jnp.roll(field * kernel_weight(offset - moved), offset, along)
    return result


def sweep_open(field, speed, padded):
    padded = padded_2(speed, (("gz", 0),), 1)
    moved = displacement(speed, padded[:-2], padded[2:])
    count = field.shape[0]
    total = jnp.zeros((count + 6,) + field.shape[1:], jnp.float32)
    for offset in range(-3, 4):
        total = total.at[3 + offset : 3 + offset + count].add(field * kernel_weight(offset - moved))
    ghosts = jnp.concatenate([total[:3], total[count + 3 :]], axis=0)
    received = padded_2(ghosts, (("gz", 0),), 3)
    result = total[3 : count + 3]
    result = result.at[:3].add(received[:3])
    result = result.at[count - 3 :].add(received[9:])
    return result


def local(scalar, velocity):
    coarse = lax.all_to_all(velocity, "gz", split_axis=1, concat_axis=3, tiled=True)
    rows_part = coarse[:1]
    next_row = passed_along(rows_part[:, :, :1, :], "gy", -1)
    y_fine = alternate(rows_part, jnp.concatenate([rows_part[:, :, 1:, :], next_row], axis=2), 2)
    fine_vel = alternate(y_fine, jnp.roll(y_fine, -1, 3), 3)
    field = sweep_periodic(scalar, fine_vel[0], 2)
    turned = jnp.swapaxes(field, 1, 2)
    padded_z = None
    sending = coarse[1:]
    field = lax.all_to_all(turned, "gy", split_axis=1, concat_axis=2, tiled=True)
    coarse_rows = jnp.swapaxes(sending, 2, 3)
    coarse_turned = lax.all_to_all(coarse_rows, "gy", split_axis=2, concat_axis=3, tiled=True)
    y_refined = alternate(coarse_turned, jnp.roll(coarse_turned, -1, 3), 3)
    next_col = passed_along(y_refined[:, :, :1, :], "gy", -1)
    pencil_vel = alternate(
        y_refined, jnp.concatenate([y_refined[:, :, 1:, :], next_col], axis=2), 2
    )
    speed_y = pencil_vel[0]
    speed_z = pencil_vel[1]
    field = sweep_periodic(field, speed_y, 2)
    return sweep_open(field, speed_z, padded_z)


def solution(mesh):
    in_specs = (P("gz", "gy", None), P(None, None, "gy", "gz"))
    out_specs = P("gz", "gy", None)
    return jax.shard_map(local, mesh=mesh, in_specs=in_specs, out_specs=out_specs, check_vma=False)
```

profile of v0, /device:TPU:0, one launch (start us, length us, event | category | flops | bytes accessed | tf_op | source)
XLA Modules:
  0.0 67.6 jit_solution(13665253573162339864)
XLA Ops:
  0.0 0.9 %copy.405 = f32[3,8,8,64]{3,2,0,1:T(8,128)S(1)} copy(f32[3,8,8,64]{3,2,1,0:T(8,128)} %param.21) | data formatting | bytes 98304 | tf_op args[1]
  1.0 8.1 %all_to_all.54 = f32[2,1,6144]{2,1,0:T(1,128)S(1)} all-to-all(f32[2,1,6144]{2,1,0:T(1,128)S(1)} %reshape.847), channel_id=1, replica_groups=mesh['gy'=16,'gz'=2] {'gz'}, dimensions={0} | all-to-all | bytes 98304 | tf_op jit(solution)/shard_map/all_to_all | solution.py:88
  9.1 0.5 broadcast.909
  9.6 0.8 %reduce.18 = f32[2,6144]{1,0:T(2,128)S(1)} reduce(f32[2,1,6144]{2,1,0:T(1,128)S(1)} %all_to_all.54, f32[]{:T(128)} %broadcast.909), dimensions={1}, to_apply=%all_to_all.39.reduce_sub_computation | reduce | bytes 98308 | tf_op jit(solution)/shard_map/all_to_all | solution.py:88
  10.7 2.7 %collective-permute-start = (f32[1,4,1,128]{3,2,1,0:T(1,128)S(1)}, f32[1,4,1,128]{3,2,1,0:T(1,128)S(1)}, u32[]{:S(2)}, u32[]{:S(2)}) collective-permute-start(f32[1,4,1,128]{3,2,1,0:T(1,128)S(1)} %slice.470), channel_id=1, source_target_pairs={{2,0},{4,2},{6,4},{8,6},{10,8},{12,10},{14,12},{16,14},{18,16},{20... | collective-permute-start | bytes 6152 | tf_op jit(solution)/shard_map/ppermute | solution.py:23
  13.6 0.3 copy.359
  13.8 1.1 %reshape.851 = f32[16,1,512]{2,1,0:T(1,128)} reshape(f32[128,2,4,8]{3,2,1,0:T(4,128)S(1)} %bitcast.81) | data formatting | bytes 65536
  15.0 3.5 %all-to-all-start.2 = ((f32[16,1,512]{2,1,0:T(1,128)}), f32[16,1,512]{2,1,0:T(1,128)S(1)}, u32[]{:S(2)}, u32[]{:S(2)}) async-start(f32[16,1,512]{2,1,0:T(1,128)} %reshape.851), calls=%async_computation.2 | async-start | bytes 65536 | tf_op jit(solution)/shard_map/all_to_all | solution.py:99
  19.0 0.3 copy.349
  19.4 0.3 copy.350
  19.8 0.3 fusion.25
  20.2 1.0 %fusion.22 = (f32[4,24,384]{2,1,0:T(8,128)S(1)}, f32[4,24,384]{2,1,0:T(8,128)S(1)}, f32[4,24,384]{2,1,0:T(8,128)S(1)}, f32[4,24,384]{2,1,0:T(8,128)S(1)}, f32[4,24,384]{2,1,0:T(8,128)S(1)}) fusion(f32[4,24,384]{2,1,0:T(8,128)S(1)} %copy-done, f32[4,24,384]{2,1,0:T(8,128)S(1)} %get-tuple-element.121), kind=kLoop, calls=%fused_computation.47 | loop fusion | flops 7741440 | bytes 1032192 | tf_op jit(solution)/shard_map/mul | solution.py:68
  21.8 0.3 fusion.16
  22.1 0.3 copy.357
  22.4 1.7 %reshape.849 = f32[16,1,2304]{2,1,0:T(1,128)} reshape(f32[384,4,24]{2,1,0:T(4,128)S(1)} %bitcast.78) | data formatting | bytes 294912
  24.1 1.0 %all-to-all-done.2 = f32[16,1,512]{2,1,0:T(1,128)S(1)} async-done(((f32[16,1,512]{2,1,0:T(1,128)}), f32[16,1,512]{2,1,0:T(1,128)S(1)}, u32[]{:S(2)}, u32[]{:S(2)}) %all-to-all-start.2) | async-done | bytes 32800 | tf_op jit(solution)/shard_map/all_to_all | solution.py:99
  25.1 4.9 %all-to-all-start.1 = ((f32[16,1,2304]{2,1,0:T(1,128)}), f32[16,1,2304]{2,1,0:T(1,128)S(1)}, u32[]{:S(2)}, u32[]{:S(2)}) async-start(f32[16,1,2304]{2,1,0:T(1,128)} %reshape.849), calls=%async_computation.1 | async-start | bytes 294912 | tf_op jit(solution)/shard_map/all_to_all | solution.py:97
  30.0 0.7 %reduce.19 = f32[16,512]{1,0:T(8,128)S(1)} reduce(f32[16,1,512]{2,1,0:T(1,128)S(1)} %all-to-all-done.2, f32[]{:T(128)} %broadcast.909), dimensions={1}, to_apply=%all_to_all.46.reduce_sub_computation | reduce | bytes 65540 | tf_op jit(solution)/shard_map/all_to_all | solution.py:99
  30.8 0.6 reshape.852
  31.4 0.3 copy.403
  31.7 0.3 all_to_all.49
  32.0 0.2 all_to_all.50
  32.4 0.7 %copy.364 = f32[2,4,8,128,3]{2,1,4,3,0:T(4,128)S(1)} copy(f32[2,4,8,128,3]{3,2,1,0,4:T(8,128)S(1)} %pad_maximum_fusion.4) | data formatting | bytes 196608 | tf_op jit(solution)/shard_map/stack | solution.py:28
  33.1 0.6 copy.366
  33.8 4.4 %collective-permute-start.1 = (f32[2,4,1,384]{3,1,2,0:T(4,128)S(1)}, f32[2,4,1,384]{3,1,2,0:T(4,128)S(1)}, u32[]{:S(2)}, u32[]{:S(2)}) collective-permute-start(f32[2,4,1,384]{3,1,2,0:T(4,128)S(1)} %copy.366), channel_id=1, source_target_pairs={{2,0},{4,2},{6,4},{8,6},{10,8},{12,10},{14,12},{16,14},{18,16},{20... | collective-permute-start | bytes 36872 | tf_op jit(solution)/shard_map/ppermute | solution.py:23
  38.2 0.9 %slice_bitcast_fusion = f32[2,4,7,1,384]{2,1,4,0,3:T(4,128)S(1)} fusion(f32[2,4,8,384]{2,1,3,0:T(4,128)S(1)} %bitcast.70), kind=kLoop, calls=%fused_computation | loop fusion | bytes 172032 | tf_op jit(solution)/shard_map/concatenate | solution.py:103
  39.1 0.6 copy.369
  39.6 0.7 copy.367
  40.5 2.2 %collective-permute-start.3 = (f32[1,24,384]{2,0,1:T(1,128)S(1)}, f32[1,24,384]{2,0,1:T(1,128)S(1)}, u32[]{:S(2)}, u32[]{:S(2)}) collective-permute-start(f32[1,24,384]{2,0,1:T(1,128)S(1)} %bitcast.97), channel_id=1, source_target_pairs={{0,1},{2,3},{4,5},{6,7},{8,9},{10,11},{12,13},{14,15},{16,17},{18,... | collective-permute-start | bytes 110600 | tf_op jit(solution)/shard_map/ppermute | solution.py:14
  42.8 1.5 %collective-permute-start.2 = (f32[1,24,384]{2,0,1:T(1,128)S(1)}, f32[1,24,384]{2,0,1:T(1,128)S(1)}, u32[]{:S(2)}, u32[]{:S(2)}) collective-permute-start(f32[1,24,384]{2,0,1:T(1,128)S(1)} %bitcast.98), channel_id=1, source_target_pairs={{1,0},{3,2},{5,4},{7,6},{9,8},{11,10},{13,12},{15,14},{17,16},{19,... | collective-permute-start | bytes 110600 | tf_op jit(solution)/shard_map/ppermute | solution.py:15
  44.7 3.9 %collective-permute-done.2 = f32[1,24,384]{2,0,1:T(1,128)S(1)} collective-permute-done((f32[1,24,384]{2,0,1:T(1,128)S(1)}, f32[1,24,384]{2,0,1:T(1,128)S(1)}, u32[]{:S(2)}, u32[]{:S(2)}) %collective-permute-start.2) | collective-permute-done | bytes 36896 | tf_op jit(solution)/shard_map/ppermute | solution.py:15
  48.6 1.0 %reduce.20 = f32[16,2304]{1,0:T(8,128)S(1)} reduce(f32[16,1,2304]{2,1,0:T(1,128)S(1)} %all-to-all-done.1, f32[]{:T(128)} %broadcast.909), dimensions={1}, to_apply=%all_to_all.42.reduce_sub_computation | reduce | bytes 294916 | tf_op jit(solution)/shard_map/all_to_all | solution.py:97
  49.6 1.1 %reshape.850 = f32[384,4,24]{2,1,0:T(4,128)S(1)} reshape(f32[16,2304]{1,0:T(8,128)S(1)} %reduce.20) | data formatting | bytes 294912
  50.7 0.5 copy.402
  51.2 0.4 all_to_all.45
  51.5 0.3 fusion.50
  51.9 1.0 %fusion.28 = (f32[4,24,384]{2,1,0:T(8,128)S(1)}, f32[4,24,384]{2,1,0:T(8,128)S(1)}, f32[4,24,384]{2,1,0:T(8,128)S(1)}, f32[4,24,384]{2,1,0:T(8,128)S(1)}, f32[4,24,384]{2,1,0:T(8,128)S(1)}) fusion(f32[4,24,384]{2,1,0:T(8,128)S(1)} %all_to_all.45, f32[4,24,384]{2,1,0:T(8,128)S(1)} %get-tuple-element.119), kind=kLoop, calls=%fused_computation.53 | loop fusion | flops 7741440 | bytes 1032192 | tf_op jit(solution)/shard_map/mul | solution.py:68
  53.5 0.6 fusion.53
  54.1 0.2 fusion.58
  54.3 0.2 fusion.63
  54.5 0.2 fusion.68
  54.7 0.2 fusion.73
  55.2 0.2 constant_dynamic-update-slice_fusion
  55.4 1.6 %collective-permute-start.4 = (f32[3,24,384]{2,1,0:T(8,128)S(1)}, f32[3,24,384]{2,1,0:T(8,128)S(1)}, u32[]{:S(2)}, u32[]{:S(2)}) collective-permute-start(f32[3,24,384]{2,1,0:T(8,128)S(1)} %slice.519), channel_id=1, source_target_pairs={{0,1},{2,3},{4,5},{6,7},{8,9},{10,11},{12,13},{14,15},{16,17},{18,... | collective-permute-start | bytes 331784 | tf_op jit(solution)/shard_map/ppermute | solution.py:14
  57.1 2.3 %collective-permute-done.4 = f32[3,24,384]{2,1,0:T(8,128)S(1)} collective-permute-done((f32[3,24,384]{2,1,0:T(8,128)S(1)}, f32[3,24,384]{2,1,0:T(8,128)S(1)}, u32[]{:S(2)}, u32[]{:S(2)}) %collective-permute-start.4) | collective-permute-done | bytes 110624 | tf_op jit(solution)/shard_map/ppermute | solution.py:14
  59.4 1.3 %collective-permute-start.5 = (f32[3,24,384]{2,1,0:T(8,128)S(1)}, f32[3,24,384]{2,1,0:T(8,128)S(1)}, u32[]{:S(2)}, u32[]{:S(2)}) collective-permute-start(f32[3,24,384]{2,1,0:T(8,128)S(1)} %get-tuple-element.122), channel_id=1, source_target_pairs={{1,0},{3,2},{5,4},{7,6},{9,8},{11,10},{13,12},{15,14},{17,16},{19,... | collective-permute-start | bytes 331784 | tf_op jit(solution)/shard_map/ppermute | solution.py:15
  60.7 5.3 %collective-permute-done.5 = f32[3,24,384]{2,1,0:T(8,128)S(1)} collective-permute-done((f32[3,24,384]{2,1,0:T(8,128)S(1)}, f32[3,24,384]{2,1,0:T(8,128)S(1)}, u32[]{:S(2)}, u32[]{:S(2)}) %collective-permute-start.5) | collective-permute-done | bytes 110624 | tf_op jit(solution)/shard_map/ppermute | solution.py:15
  66.0 1.6 %fusion.226 = f32[4,24,384]{2,1,0:T(8,128)} fusion(f32[4,24,384]{2,1,0:T(8,128)} %copy-done.1, f32[3,24,384]{2,1,0:T(8,128)S(1)} %collective-permute-done.5), kind=kLoop, calls=%fused_computation.310 | loop fusion | flops 27648 | bytes 331776 | tf_op jit(solution)/shard_map/scatter-add | solution.py:83
  (73 shorter events, 3.4 us)
Async XLA Ops:
  10.7 7.8 %collective-permute-start = (f32[1,4,1,128]{3,2,1,0:T(1,128)S(1)}, f32[1,4,1,128]{3,2,1,0:T(1,128)S(1)}, u32[]{:S(2)}, u32[]{:S(2)}) collective-permute-start(f32[1,4,1,128]{3,2,1,0:T(1,128)S(1)} %slice.470), channel_id=1, source_target_pairs={{2,0},{4,2},{6,4},{8,6},{10,8},{12,10},{14,12},{16,14},{18,16},{20... | collective-permute-start | bytes 6152 | tf_op jit(solution)/shard_map/ppermute | solution.py:23
  15.0 10.1 %all-to-all-start.2 = ((f32[16,1,512]{2,1,0:T(1,128)}), f32[16,1,512]{2,1,0:T(1,128)S(1)}, u32[]{:S(2)}, u32[]{:S(2)}) async-start(f32[16,1,512]{2,1,0:T(1,128)} %reshape.851), calls=%async_computation.2 | async-start | bytes 65536 | tf_op jit(solution)/shard_map/all_to_all | solution.py:99
  18.9 1.0 %copy-start = (f32[4,24,384]{2,1,0:T(8,128)S(1)}, f32[4,24,384]{2,1,0:T(8,128)}, u32[]{:S(2)}) copy-start(f32[4,24,384]{2,1,0:T(8,128)} %param.20) | copy-start | bytes 442372
  25.1 23.6 %all-to-all-start.1 = ((f32[16,1,2304]{2,1,0:T(1,128)}), f32[16,1,2304]{2,1,0:T(1,128)S(1)}, u32[]{:S(2)}, u32[]{:S(2)}) async-start(f32[16,1,2304]{2,1,0:T(1,128)} %reshape.849), calls=%async_computation.1 | async-start | bytes 294912 | tf_op jit(solution)/shard_map/all_to_all | solution.py:97
  33.8 6.5 %collective-permute-start.1 = (f32[2,4,1,384]{3,1,2,0:T(4,128)S(1)}, f32[2,4,1,384]{3,1,2,0:T(4,128)S(1)}, u32[]{:S(2)}, u32[]{:S(2)}) collective-permute-start(f32[2,4,1,384]{3,1,2,0:T(4,128)S(1)} %copy.366), channel_id=1, source_target_pairs={{2,0},{4,2},{6,4},{8,6},{10,8},{12,10},{14,12},{16,14},{18,16},{20... | collective-permute-start | bytes 36872 | tf_op jit(solution)/shard_map/ppermute | solution.py:23
  40.5 4.2 %collective-permute-start.3 = (f32[1,24,384]{2,0,1:T(1,128)S(1)}, f32[1,24,384]{2,0,1:T(1,128)S(1)}, u32[]{:S(2)}, u32[]{:S(2)}) collective-permute-start(f32[1,24,384]{2,0,1:T(1,128)S(1)} %bitcast.97), channel_id=1, source_target_pairs={{0,1},{2,3},{4,5},{6,7},{8,9},{10,11},{12,13},{14,15},{16,17},{18,... | collective-permute-start | bytes 110600 | tf_op jit(solution)/shard_map/ppermute | solution.py:14
  42.8 5.9 %collective-permute-start.2 = (f32[1,24,384]{2,0,1:T(1,128)S(1)}, f32[1,24,384]{2,0,1:T(1,128)S(1)}, u32[]{:S(2)}, u32[]{:S(2)}) collective-permute-start(f32[1,24,384]{2,0,1:T(1,128)S(1)} %bitcast.98), channel_id=1, source_target_pairs={{1,0},{3,2},{5,4},{7,6},{9,8},{11,10},{13,12},{15,14},{17,16},{19,... | collective-permute-start | bytes 110600 | tf_op jit(solution)/shard_map/ppermute | solution.py:15
  55.4 3.9 %collective-permute-start.4 = (f32[3,24,384]{2,1,0:T(8,128)S(1)}, f32[3,24,384]{2,1,0:T(8,128)S(1)}, u32[]{:S(2)}, u32[]{:S(2)}) collective-permute-start(f32[3,24,384]{2,1,0:T(8,128)S(1)} %slice.519), channel_id=1, source_target_pairs={{0,1},{2,3},{4,5},{6,7},{8,9},{10,11},{12,13},{14,15},{16,17},{18,... | collective-permute-start | bytes 331784 | tf_op jit(solution)/shard_map/ppermute | solution.py:14
  59.4 6.7 %copy-start.1 = (f32[4,24,384]{2,1,0:T(8,128)}, f32[4,24,384]{2,1,0:T(8,128)S(1)}, u32[]{:S(2)}) copy-start(f32[4,24,384]{2,1,0:T(8,128)S(1)} %get-tuple-element.123) | copy-start | bytes 442372
  59.4 6.6 %collective-permute-start.5 = (f32[3,24,384]{2,1,0:T(8,128)S(1)}, f32[3,24,384]{2,1,0:T(8,128)S(1)}, u32[]{:S(2)}, u32[]{:S(2)}) collective-permute-start(f32[3,24,384]{2,1,0:T(8,128)S(1)} %get-tuple-element.122), channel_id=1, source_target_pairs={{1,0},{3,2},{5,4},{7,6},{9,8},{11,10},{13,12},{15,14},{17,16},{19,... | collective-permute-start | bytes 331784 | tf_op jit(solution)/shard_map/ppermute | solution.py:15
where the time goes:
time: 68 us; the launch traced here: 67.6 us
  starting transfers between devices  22.1 us (32%)
  local copies, waits for them, and re-layouts  15.1 us (22%)
  waiting for transfers between devices  12.6 us (19%)
  other arithmetic  9.22 us (14%)
  blocking collectives  8.07 us (12%)
    ppermute x2, waiting for transfers between devices, padded_2(): after = lax.ppermute(initial, axis, down)  9.27 us
    all_to_all x1, blocking collectives, local(): lax.all_to_all(velocity, 'gz', split_axis=1, concat_axis=3, tiled=True)  8.07 us
    ppermute x2, starting transfers between devices, passed_along(): return lax.ppermute(block, axis, route)  7.05 us
    unnamed x15, local copies, waits for them, and re-layouts  5.7 us
    all_to_all x1, starting transfers between devices, local(): lax.all_to_all(turned, 'gy', split_axis=1, concat_axis=2, tiled=True)  4.95 us
    ppermute x2, starting transfers between devices, padded_2(): before = lax.ppermute(last, axis, up)  3.81 us
    all_to_all x1, starting transfers between devices, local(): lax.all_to_all(coarse_rows, 'gy', split_axis=2, concat_axis=3, tiled=True)  3.49 us
    ppermute x2, starting transfers between devices, padded_2(): after = lax.ppermute(initial, axis, down)  2.76 us
  transfers between devices with their start and end apart: 8, of which 4 were waited for; matrix products, arithmetic and copies ran while one was open for 19% of the time, Pallas kernels for 0%

commit v1 on v0

--- a/solution.py
+++ b/solution.py
@@ -96,7 +96,11 @@
     sending = coarse[1:]
     field = lax.all_to_all(turned, "gy", split_axis=1, concat_axis=2, tiled=True)
     coarse_rows = jnp.swapaxes(sending, 2, 3)
-    coarse_turned = lax.all_to_all(coarse_rows, "gy", split_axis=2, concat_axis=3, tiled=True)
+    y = lax.axis_size("gy")
+    block_next = jnp.split(coarse_rows, y, axis=2)
+    raw_out = jnp.stack(block_next)
+    carry_out = lax.all_to_all(raw_out, axis_name="gy", split_axis=0, concat_axis=0)
+    coarse_turned = jnp.concatenate(carry_out, axis=3)
     y_refined = alternate(coarse_turned, jnp.roll(coarse_turned, -1, 3), 3)
     next_col = passed_along(y_refined[:, :, :1, :], "gy", -1)
     pencil_vel = alternate(

time: 68 us -> 68.4 us (level)
    reshape x0 -> x4, local copies, waits for them, and re-layouts: none -> 0.82 us  [local(): coarse_turned = jnp.concatenate(carry_out, axis=3)]
    all_to_all x3 -> x0, local copies, waits for them, and re-layouts: 0.81 us -> none  [local(): lax.all_to_all(coarse_rows, 'gy', split_axis=2, concat_axis=3, tiled=True)]
    unnamed x15 -> x30, local copies, waits for them, and re-layouts: 5.7 us -> 6.19 us
  transfers between devices with their start and end apart: 8 -> 8, of which waited for: 4 -> 4; matrix products, arithmetic and copies ran while one was open for 19% -> 18% of each run, Pallas kernels for 0% -> 0%
where the time goes in v1:
time: 68.4 us; the launch traced here: 67.9 us
  starting transfers between devices  22.1 us (32%)
  local copies, waits for them, and re-layouts  15.4 us (23%)
  waiting for transfers between devices  12.6 us (18%)
  other arithmetic  9.22 us (13%)
  blocking collectives  8.07 us (12%)
    ppermute x2, waiting for transfers between devices, padded_2(): after = lax.ppermute(initial, axis, down)  9.27 us
    all_to_all x1, blocking collectives, local(): lax.all_to_all(velocity, 'gz', split_axis=1, concat_axis=3, tiled=True)  8.07 us
    ppermute x2, starting transfers between devices, passed_along(): return lax.ppermute(block, axis, route)  7.05 us
    unnamed x30, local copies, waits for them, and re-layouts  6.19 us
    all_to_all x1, starting transfers between devices, local(): lax.all_to_all(turned, 'gy', split_axis=1, concat_axis=2, tiled=True)  4.95 us
    ppermute x2, starting transfers between devices, padded_2(): before = lax.ppermute(last, axis, up)  3.81 us
    all_to_all x1, starting transfers between devices, local(): lax.all_to_all(raw_out, axis_name='gy', split_axis=0, concat_axis=0)  3.49 us
    ppermute x2, starting transfers between devices, padded_2(): after = lax.ppermute(initial, axis, down)  2.76 us
  transfers between devices with their start and end apart: 8, of which 4 were waited for; matrix products, arithmetic and copies ran while one was open for 18% of the time, Pallas kernels for 0%

profile of v1, /device:TPU:0, one launch (start us, length us, event | category | flops | bytes accessed | tf_op | source)
XLA Modules:
  0.0 67.9 jit_solution(13473637090510232205)
XLA Ops:
  0.0 0.9 %copy.393 = f32[3,8,8,64]{3,2,0,1:T(8,128)S(1)} copy(f32[3,8,8,64]{3,2,1,0:T(8,128)} %param.21) | data formatting | bytes 98304 | tf_op args[1]
  1.0 8.1 %all_to_all.38 = f32[2,1,6144]{2,1,0:T(1,128)S(1)} all-to-all(f32[2,1,6144]{2,1,0:T(1,128)S(1)} %reshape.858), channel_id=1, replica_groups=mesh['gy'=16,'gz'=2] {'gz'}, dimensions={0} | all-to-all | bytes 98304 | tf_op jit(solution)/shard_map/all_to_all | solution.py:88
  9.1 0.5 broadcast.909
  9.6 0.8 %reduce.18 = f32[2,6144]{1,0:T(2,128)S(1)} reduce(f32[2,1,6144]{2,1,0:T(1,128)S(1)} %all_to_all.38, f32[]{:T(128)} %broadcast.909), dimensions={1}, to_apply=%all_to_all.27.reduce_sub_computation | reduce | bytes 98308 | tf_op jit(solution)/shard_map/all_to_all | solution.py:88
  12.0 2.7 %collective-permute-start = (f32[1,4,1,128]{3,2,1,0:T(1,128)S(1)}, f32[1,4,1,128]{3,2,1,0:T(1,128)S(1)}, u32[]{:S(2)}, u32[]{:S(2)}) collective-permute-start(f32[1,4,1,128]{3,2,1,0:T(1,128)S(1)} %slice.470), channel_id=1, source_target_pairs={{2,0},{4,2},{6,4},{8,6},{10,8},{12,10},{14,12},{16,14},{18,16},{20... | collective-permute-start | bytes 6152 | tf_op jit(solution)/shard_map/ppermute | solution.py:23
  14.8 0.9 %reshape.862 = f32[16,1,512]{2,1,0:T(1,128)} reshape(f32[16,2,4,8,8]{4,3,2,1,0:T(8,128)S(1)} %bitcast.165) | data formatting | bytes 65536
  15.7 3.5 %all-to-all-start.2 = ((f32[16,1,512]{2,1,0:T(1,128)}), f32[16,1,512]{2,1,0:T(1,128)S(1)}, u32[]{:S(2)}, u32[]{:S(2)}) async-start(f32[16,1,512]{2,1,0:T(1,128)} %reshape.862), calls=%async_computation.2 | async-start | bytes 65536 | tf_op jit(solution)/shard_map/all_to_all | solution.py:102
  19.7 0.3 copy.343
  20.0 0.3 copy.344
  20.5 0.3 fusion.25
  20.8 1.0 %fusion.22 = (f32[4,24,384]{2,1,0:T(8,128)S(1)}, f32[4,24,384]{2,1,0:T(8,128)S(1)}, f32[4,24,384]{2,1,0:T(8,128)S(1)}, f32[4,24,384]{2,1,0:T(8,128)S(1)}, f32[4,24,384]{2,1,0:T(8,128)S(1)}) fusion(f32[4,24,384]{2,1,0:T(8,128)S(1)} %copy-done, f32[4,24,384]{2,1,0:T(8,128)S(1)} %get-tuple-element.121), kind=kLoop, calls=%fused_computation.46 | loop fusion | flops 7741440 | bytes 1032192 | tf_op jit(solution)/shard_map/mul | solution.py:68
  22.4 0.3 fusion.16
  22.7 0.3 copy.351
  23.1 1.7 %reshape.860 = f32[16,1,2304]{2,1,0:T(1,128)} reshape(f32[384,4,24]{2,1,0:T(4,128)S(1)} %bitcast.154) | data formatting | bytes 294912
  24.7 1.0 %all-to-all-done.2 = f32[16,1,512]{2,1,0:T(1,128)S(1)} async-done(((f32[16,1,512]{2,1,0:T(1,128)}), f32[16,1,512]{2,1,0:T(1,128)S(1)}, u32[]{:S(2)}, u32[]{:S(2)}) %all-to-all-start.2) | async-done | bytes 32800 | tf_op jit(solution)/shard_map/all_to_all | solution.py:102
  25.8 4.9 %all-to-all-start.1 = ((f32[16,1,2304]{2,1,0:T(1,128)}), f32[16,1,2304]{2,1,0:T(1,128)S(1)}, u32[]{:S(2)}, u32[]{:S(2)}) async-start(f32[16,1,2304]{2,1,0:T(1,128)} %reshape.860), calls=%async_computation.1 | async-start | bytes 294912 | tf_op jit(solution)/shard_map/all_to_all | solution.py:97
  30.7 0.7 %reduce.19 = f32[16,512]{1,0:T(8,128)S(1)} reduce(f32[16,1,512]{2,1,0:T(1,128)S(1)} %all-to-all-done.2, f32[]{:T(128)} %broadcast.909), dimensions={1}, to_apply=%all_to_all.34.reduce_sub_computation | reduce | bytes 65540 | tf_op jit(solution)/shard_map/all_to_all | solution.py:102
  31.4 0.3 reshape.863
  31.8 0.3 copy.353
  32.1 0.3 reshape.854
  32.3 0.2 reshape.855
  32.8 0.7 %copy.356 = f32[2,4,8,128,3]{2,1,4,3,0:T(4,128)S(1)} copy(f32[2,4,8,128,3]{3,2,1,0,4:T(8,128)S(1)} %pad_maximum_fusion.4) | data formatting | bytes 196608 | tf_op jit(solution)/shard_map/stack | solution.py:28
  33.5 0.6 copy.358
  34.1 4.4 %collective-permute-start.1 = (f32[2,4,1,384]{3,1,2,0:T(4,128)S(1)}, f32[2,4,1,384]{3,1,2,0:T(4,128)S(1)}, u32[]{:S(2)}, u32[]{:S(2)}) collective-permute-start(f32[2,4,1,384]{3,1,2,0:T(4,128)S(1)} %copy.358), channel_id=1, source_target_pairs={{2,0},{4,2},{6,4},{8,6},{10,8},{12,10},{14,12},{16,14},{18,16},{20... | collective-permute-start | bytes 36872 | tf_op jit(solution)/shard_map/ppermute | solution.py:23
  38.5 0.9 %slice_bitcast_fusion = f32[2,4,7,1,384]{2,1,4,0,3:T(4,128)S(1)} fusion(f32[2,4,8,384]{2,1,3,0:T(4,128)S(1)} %bitcast.132), kind=kLoop, calls=%fused_computation | loop fusion | bytes 172032 | tf_op jit(solution)/shard_map/concatenate | solution.py:107
  39.4 0.6 copy.361
  40.0 0.7 copy.359
  40.9 2.2 %collective-permute-start.3 = (f32[1,24,384]{2,0,1:T(1,128)S(1)}, f32[1,24,384]{2,0,1:T(1,128)S(1)}, u32[]{:S(2)}, u32[]{:S(2)}) collective-permute-start(f32[1,24,384]{2,0,1:T(1,128)S(1)} %bitcast.171), channel_id=1, source_target_pairs={{0,1},{2,3},{4,5},{6,7},{8,9},{10,11},{12,13},{14,15},{16,17},{18,... | collective-permute-start | bytes 110600 | tf_op jit(solution)/shard_map/ppermute | solution.py:14
  43.1 1.5 %collective-permute-start.2 = (f32[1,24,384]{2,0,1:T(1,128)S(1)}, f32[1,24,384]{2,0,1:T(1,128)S(1)}, u32[]{:S(2)}, u32[]{:S(2)}) collective-permute-start(f32[1,24,384]{2,0,1:T(1,128)S(1)} %bitcast.172), channel_id=1, source_target_pairs={{1,0},{3,2},{5,4},{7,6},{9,8},{11,10},{13,12},{15,14},{17,16},{19,... | collective-permute-start | bytes 110600 | tf_op jit(solution)/shard_map/ppermute | solution.py:15
  45.0 3.9 %collective-permute-done.2 = f32[1,24,384]{2,0,1:T(1,128)S(1)} collective-permute-done((f32[1,24,384]{2,0,1:T(1,128)S(1)}, f32[1,24,384]{2,0,1:T(1,128)S(1)}, u32[]{:S(2)}, u32[]{:S(2)}) %collective-permute-start.2) | collective-permute-done | bytes 36896 | tf_op jit(solution)/shard_map/ppermute | solution.py:15
  49.0 1.0 %reduce.20 = f32[16,2304]{1,0:T(8,128)S(1)} reduce(f32[16,1,2304]{2,1,0:T(1,128)S(1)} %all-to-all-done.1, f32[]{:T(128)} %broadcast.909), dimensions={1}, to_apply=%all_to_all.30.reduce_sub_computation | reduce | bytes 294916 | tf_op jit(solution)/shard_map/all_to_all | solution.py:97
  50.0 1.1 %reshape.861 = f32[384,4,24]{2,1,0:T(4,128)S(1)} reshape(f32[16,2304]{1,0:T(8,128)S(1)} %reduce.20) | data formatting | bytes 294912
  51.0 0.5 copy.391
  51.5 0.4 all_to_all.33
  51.9 0.3 fusion.50
  52.2 1.0 %fusion.28 = (f32[4,24,384]{2,1,0:T(8,128)S(1)}, f32[4,24,384]{2,1,0:T(8,128)S(1)}, f32[4,24,384]{2,1,0:T(8,128)S(1)}, f32[4,24,384]{2,1,0:T(8,128)S(1)}, f32[4,24,384]{2,1,0:T(8,128)S(1)}) fusion(f32[4,24,384]{2,1,0:T(8,128)S(1)} %all_to_all.33, f32[4,24,384]{2,1,0:T(8,128)S(1)} %get-tuple-element.119), kind=kLoop, calls=%fused_computation.52 | loop fusion | flops 7741440 | bytes 1032192 | tf_op jit(solution)/shard_map/mul | solution.py:68
  53.8 0.6 fusion.53
  54.4 0.2 fusion.58
  54.6 0.2 fusion.63
  54.9 0.2 fusion.68
  55.1 0.2 fusion.73
  55.3 0.2 fusion.78
  55.5 0.2 constant_dynamic-update-slice_fusion.16
  55.8 1.6 %collective-permute-start.4 = (f32[3,24,384]{2,1,0:T(8,128)S(1)}, f32[3,24,384]{2,1,0:T(8,128)S(1)}, u32[]{:S(2)}, u32[]{:S(2)}) collective-permute-start(f32[3,24,384]{2,1,0:T(8,128)S(1)} %slice.519), channel_id=1, source_target_pairs={{0,1},{2,3},{4,5},{6,7},{8,9},{10,11},{12,13},{14,15},{16,17},{18,... | collective-permute-start | bytes 331784 | tf_op jit(solution)/shard_map/ppermute | solution.py:14
  57.4 2.3 %collective-permute-done.4 = f32[3,24,384]{2,1,0:T(8,128)S(1)} collective-permute-done((f32[3,24,384]{2,1,0:T(8,128)S(1)}, f32[3,24,384]{2,1,0:T(8,128)S(1)}, u32[]{:S(2)}, u32[]{:S(2)}) %collective-permute-start.4) | collective-permute-done | bytes 110624 | tf_op jit(solution)/shard_map/ppermute | solution.py:14
  59.7 1.3 %collective-permute-start.5 = (f32[3,24,384]{2,1,0:T(8,128)S(1)}, f32[3,24,384]{2,1,0:T(8,128)S(1)}, u32[]{:S(2)}, u32[]{:S(2)}) collective-permute-start(f32[3,24,384]{2,1,0:T(8,128)S(1)} %get-tuple-element.122), channel_id=1, source_target_pairs={{1,0},{3,2},{5,4},{7,6},{9,8},{11,10},{13,12},{15,14},{17,16},{19,... | collective-permute-start | bytes 331784 | tf_op jit(solution)/shard_map/ppermute | solution.py:15
  61.0 5.3 %collective-permute-done.5 = f32[3,24,384]{2,1,0:T(8,128)S(1)} collective-permute-done((f32[3,24,384]{2,1,0:T(8,128)S(1)}, f32[3,24,384]{2,1,0:T(8,128)S(1)}, u32[]{:S(2)}, u32[]{:S(2)}) %collective-permute-start.5) | collective-permute-done | bytes 110624 | tf_op jit(solution)/shard_map/ppermute | solution.py:15
  66.4 1.6 %fusion.226 = f32[4,24,384]{2,1,0:T(8,128)} fusion(f32[4,24,384]{2,1,0:T(8,128)} %copy-done.1, f32[3,24,384]{2,1,0:T(8,128)S(1)} %collective-permute-done.5), kind=kLoop, calls=%fused_computation.309 | loop fusion | flops 27648 | bytes 331776 | tf_op jit(solution)/shard_map/scatter-add | solution.py:83
  (89 shorter events, 4.4 us)
Async XLA Ops:
  12.0 7.2 %collective-permute-start = (f32[1,4,1,128]{3,2,1,0:T(1,128)S(1)}, f32[1,4,1,128]{3,2,1,0:T(1,128)S(1)}, u32[]{:S(2)}, u32[]{:S(2)}) collective-permute-start(f32[1,4,1,128]{3,2,1,0:T(1,128)S(1)} %slice.470), channel_id=1, source_target_pairs={{2,0},{4,2},{6,4},{8,6},{10,8},{12,10},{14,12},{16,14},{18,16},{20... | collective-permute-start | bytes 6152 | tf_op jit(solution)/shard_map/ppermute | solution.py:23
  15.7 10.1 %all-to-all-start.2 = ((f32[16,1,512]{2,1,0:T(1,128)}), f32[16,1,512]{2,1,0:T(1,128)S(1)}, u32[]{:S(2)}, u32[]{:S(2)}) async-start(f32[16,1,512]{2,1,0:T(1,128)} %reshape.862), calls=%async_computation.2 | async-start | bytes 65536 | tf_op jit(solution)/shard_map/all_to_all | solution.py:102
  19.5 1.0 %copy-start = (f32[4,24,384]{2,1,0:T(8,128)S(1)}, f32[4,24,384]{2,1,0:T(8,128)}, u32[]{:S(2)}) copy-start(f32[4,24,384]{2,1,0:T(8,128)} %param.20) | copy-start | bytes 442372
  25.8 23.2 %all-to-all-start.1 = ((f32[16,1,2304]{2,1,0:T(1,128)}), f32[16,1,2304]{2,1,0:T(1,128)S(1)}, u32[]{:S(2)}, u32[]{:S(2)}) async-start(f32[16,1,2304]{2,1,0:T(1,128)} %reshape.860), calls=%async_computation.1 | async-start | bytes 294912 | tf_op jit(solution)/shard_map/all_to_all | solution.py:97
  34.1 6.5 %collective-permute-start.1 = (f32[2,4,1,384]{3,1,2,0:T(4,128)S(1)}, f32[2,4,1,384]{3,1,2,0:T(4,128)S(1)}, u32[]{:S(2)}, u32[]{:S(2)}) collective-permute-start(f32[2,4,1,384]{3,1,2,0:T(4,128)S(1)} %copy.358), channel_id=1, source_target_pairs={{2,0},{4,2},{6,4},{8,6},{10,8},{12,10},{14,12},{16,14},{18,16},{20... | collective-permute-start | bytes 36872 | tf_op jit(solution)/shard_map/ppermute | solution.py:23
  40.9 4.2 %collective-permute-start.3 = (f32[1,24,384]{2,0,1:T(1,128)S(1)}, f32[1,24,384]{2,0,1:T(1,128)S(1)}, u32[]{:S(2)}, u32[]{:S(2)}) collective-permute-start(f32[1,24,384]{2,0,1:T(1,128)S(1)} %bitcast.171), channel_id=1, source_target_pairs={{0,1},{2,3},{4,5},{6,7},{8,9},{10,11},{12,13},{14,15},{16,17},{18,... | collective-permute-start | bytes 110600 | tf_op jit(solution)/shard_map/ppermute | solution.py:14
  43.1 5.9 %collective-permute-start.2 = (f32[1,24,384]{2,0,1:T(1,128)S(1)}, f32[1,24,384]{2,0,1:T(1,128)S(1)}, u32[]{:S(2)}, u32[]{:S(2)}) collective-permute-start(f32[1,24,384]{2,0,1:T(1,128)S(1)} %bitcast.172), channel_id=1, source_target_pairs={{1,0},{3,2},{5,4},{7,6},{9,8},{11,10},{13,12},{15,14},{17,16},{19,... | collective-permute-start | bytes 110600 | tf_op jit(solution)/shard_map/ppermute | solution.py:15
  55.8 3.9 %collective-permute-start.4 = (f32[3,24,384]{2,1,0:T(8,128)S(1)}, f32[3,24,384]{2,1,0:T(8,128)S(1)}, u32[]{:S(2)}, u32[]{:S(2)}) collective-permute-start(f32[3,24,384]{2,1,0:T(8,128)S(1)} %slice.519), channel_id=1, source_target_pairs={{0,1},{2,3},{4,5},{6,7},{8,9},{10,11},{12,13},{14,15},{16,17},{18,... | collective-permute-start | bytes 331784 | tf_op jit(solution)/shard_map/ppermute | solution.py:14
  59.7 6.7 %copy-start.1 = (f32[4,24,384]{2,1,0:T(8,128)}, f32[4,24,384]{2,1,0:T(8,128)S(1)}, u32[]{:S(2)}) copy-start(f32[4,24,384]{2,1,0:T(8,128)S(1)} %get-tuple-element.123) | copy-start | bytes 442372
  59.7 6.6 %collective-permute-start.5 = (f32[3,24,384]{2,1,0:T(8,128)S(1)}, f32[3,24,384]{2,1,0:T(8,128)S(1)}, u32[]{:S(2)}, u32[]{:S(2)}) collective-permute-start(f32[3,24,384]{2,1,0:T(8,128)S(1)} %get-tuple-element.122), channel_id=1, source_target_pairs={{1,0},{3,2},{5,4},{7,6},{9,8},{11,10},{13,12},{15,14},{17,16},{19,... | collective-permute-start | bytes 331784 | tf_op jit(solution)/shard_map/ppermute | solution.py:15
